TPU v7x, 32 devices: a whole 2x2x4 slice. The times are simulated.
32 devices in a mesh: fsdp: 8 (over z, core), chan: 4 (over y, x).
Axes of the slice: x: 2, y: 2, z: 4, core: 2. Of those that a mesh axis runs over, the one named last changes fastest.
Arguments:
- in_master: float32 [4096, 2, 4096], P(('fsdp', 'chan')), may hold values from -0.09375 to 0.09375
- in_moment: float32 [4096, 2, 4096], P(('fsdp', 'chan')), may hold values from -1.8 to 1.8
- in_velocity: float32 [4096, 2, 4096], P(('fsdp', 'chan')), may hold values from 0.05 to 1
- in_grad: bfloat16 [4096, 2, 4096], P(('fsdp', 'chan')), may hold values from -6 to 6
- out_master: float32 [4096, 4096], P(('fsdp', 'chan')), may hold values from -0.09375 to 0.09375
- out_moment: float32 [4096, 4096], P(('fsdp', 'chan')), may hold values from -1.8 to 1.8
- out_velocity: float32 [4096, 4096], P(('fsdp', 'chan')), may hold values from 0.001 to 1
- out_grad: bfloat16 [4096, 4096], P(('fsdp', 'chan')), may hold values from -6 to 6
- embed_table: bfloat16 [65536, 4096], P('fsdp', 'chan'), may hold values from -18 to 18
- tokens: int32 [4, 1024], P(None, 'fsdp'), may hold values from 0 to 65535, as said below
- conv_state: bfloat16 [1024, 3, 4096], P('fsdp', None, 'chan'), may hold values from -6 to 6
- ssm_state: float32 [1024, 16, 4096], P('fsdp', None, 'chan'), may hold values from -6 to 6
- conv_weight: float32 [4, 4096], P(None, 'chan'), may hold values from -3 to 3
- conv_bias: float32 [4096], P('chan'), may hold values from -3 to 3
- x_proj_w: bfloat16 [288, 4096], P(None, 'chan'), may hold values from -0.09375 to 0.09375
- dt_proj_w: bfloat16 [4096, 256], P('chan'), may hold values from -0.375 to 0.375
- dt_bias: float32 [4096], P('chan'), may hold values from -4.5 to -2
- a_log: float32 [16, 4096], P(None, 'chan'), may hold values from 0 to 2.77
- d_skip: float32 [4096], P('chan'), may hold values from 0.5 to 2
Outputs:
- in_master_new: float32 [4096, 2, 4096], P(('fsdp', 'chan'))
- out_master_new: float32 [4096, 4096], P(('fsdp', 'chan'))
- block_out: bfloat16 [4, 1024, 4096], P(None, 'fsdp', 'chan')
- conv_state_new: bfloat16 [1024, 3, 4096], P('fsdp', None, 'chan')
- ssm_state_new: float32 [1024, 16, 4096], P('fsdp', None, 'chan')
Inputs may be any that keep to these rules, and one draw needn't show every extreme that they name: Split the ids into 8 equal consecutive vocabulary blocks and the sequences into 8 equal consecutive replicas; of one replica's 4 x 128 tokens at most 128 lie in any one block, and some block holds exactly 128 of them.
All inputs are finite; a program needn't handle non-finite values.
Results may differ from a plain program's by a relative error of at most 0.012.
Values may be sent and summed in bfloat16 or wider, within the bound.
A program may use at most 192 MiB of HBM per device.

v0:
```python
import math
import jax
import jax.numpy as jnp
from jax import lax
from jax.sharding import PartitionSpec as P

RANK = 256
NSTATE = 16
learn_rate = 0.01
beta_first = 0.8
beta_second = 0.95
adam_eps = 1e-08
weight_decay = 0.1
bias_first = 1.0 - math.pow(0.8, 10)
bias_second = 1.0 - math.pow(0.95, 10)
norm_eps = 1e-06


def adam_update(master, moment, velocity, grad):
    gradient = grad.astype(jnp.float32)
    moment = beta_first * moment + (1.0 - beta_first) * gradient
    velocity = beta_second * velocity + (1.0 - beta_second) * gradient * gradient
    update = moment / bias_first / (jnp.sqrt(velocity / bias_second) + adam_eps)
    return master - learn_rate * (update + weight_decay * master)


def reorder_rows(block, groups, replicas):
    width = block.shape[1]
    shaped = block.reshape(groups, replicas, -1, width)
    return jnp.transpose(shaped, (1, 0, 2, 3)).reshape(-1, width)


def per_device(
    in_master,
    in_moment,
    in_velocity,
    in_grad,
    out_master,
    out_moment,
    out_velocity,
    out_grad,
    embed_table,
    tokens,
    conv_state,
    ssm_state,
    conv_weight,
    conv_bias,
    x_proj_w,
    dt_proj_w,
    dt_bias,
    a_log,
    d_skip,
):
    in_new = adam_update(in_master, in_moment, in_velocity, in_grad)
    out_new = adam_update(out_master, out_moment, out_velocity, out_grad)
    pieces = (
        in_new[:, 0, :].astype(jnp.bfloat16),
        in_new[:, 1, :].astype(jnp.bfloat16),
        out_new.astype(jnp.bfloat16),
    )
    groups = lax.axis_size("chan")
    replicas = lax.axis_size("fsdp")
    stacked = (
        lax.all_gather(pieces[0], "fsdp", axis=0, tiled=True),
        lax.all_gather(pieces[1], "fsdp", axis=0, tiled=True),
        lax.all_gather(pieces[2], "fsdp", axis=0, tiled=True),
    )
    spread = (
        lax.all_to_all(stacked[0], "chan", split_axis=1, concat_axis=0, tiled=True),
        lax.all_to_all(stacked[1], "chan", split_axis=1, concat_axis=0, tiled=True),
        lax.all_to_all(stacked[2], "chan", split_axis=1, concat_axis=0, tiled=True),
    )
    relay_x = reorder_rows(spread[0], groups, replicas)
    relay_z = reorder_rows(spread[1], groups, replicas)
    relay_out = reorder_rows(spread[2], groups, replicas)
    vocab_rows = embed_table.shape[0]
    every_token = lax.all_gather(tokens, "fsdp", axis=1, tiled=True)
    offset = every_token - lax.axis_index("fsdp") * vocab_rows
    inside = jnp.logical_and(offset >= 0, offset < vocab_rows)
    picked = jnp.take(embed_table, jnp.clip(offset, 0, vocab_rows - 1), axis=0)
    picked = jnp.where(inside[:, :, None], picked, jnp.zeros((), jnp.bfloat16))
    found = (
        lax.psum_scatter(picked, "fsdp", scatter_dimension=1, tiled=True)
        .astype(jnp.float32)
        .astype(jnp.bfloat16)
    )
    inputs = lax.all_gather(found, "chan", axis=2, tiled=True)
    steps, rows, width = inputs.shape
    flat = inputs.reshape(steps * rows, width).astype(jnp.float32)
    normed = (flat * lax.rsqrt(jnp.mean(flat * flat, axis=1, keepdims=True) + norm_eps)).astype(
        jnp.bfloat16
    )
    x_in = (
        jnp.dot(normed, relay_x, preferred_element_type=jnp.float32)
        .astype(jnp.bfloat16)
        .reshape(steps, rows, -1)
    )
    z_in = (
        jnp.dot(normed, relay_z, preferred_element_type=jnp.float32)
        .astype(jnp.bfloat16)
        .reshape(steps, rows, -1)
    )
    decay = -jnp.exp(a_log)
    contract_last = (((1,), (1,)), ((), ()))
    window_state = conv_state
    state = ssm_state
    gates = []
    for step in range(steps):
        window = jnp.concatenate([window_state, x_in[step][:, None, :]], axis=1)
        mixed_conv = jnp.sum(window.astype(jnp.float32) * conv_weight[None], axis=1) + conv_bias
        act = jax.nn.silu(mixed_conv).astype(jnp.bfloat16)
        partial_value = lax.dot_general(
            act, x_proj_w, contract_last, preferred_element_type=jnp.float32
        )
        dbc = lax.psum(partial_value, "chan")
        dt_low = dbc[:, :RANK].astype(jnp.bfloat16)
        b_mat = dbc[:, RANK : RANK + NSTATE]
        c_mat = dbc[:, RANK + NSTATE :]
        delta = jax.nn.softplus(
            lax.dot_general(dt_low, dt_proj_w, contract_last, preferred_element_type=jnp.float32)
            + dt_bias
        )
        act_real = act.astype(jnp.float32)
        state = (
            jnp.exp(delta[:, None, :] * decay[None]) * state
            + (delta * act_real)[:, None, :] * b_mat[:, :, None]
        )
        y_out = jnp.sum(c_mat[:, :, None] * state, axis=1) + d_skip * act_real
        gated = (y_out * jax.nn.silu(z_in[step].astype(jnp.float32))).astype(jnp.bfloat16)
        gates.append(gated)
        window_state = window[:, 1:, :]
    stacked_gates = jnp.stack(gates)
    terms = lax.dot_general(
        stacked_gates, relay_out, (((2,), (1,)), ((), ())), preferred_element_type=jnp.float32
    )
    mixed_all = lax.psum_scatter(
        terms.astype(jnp.bfloat16), "chan", scatter_dimension=2, tiled=True
    ).astype(jnp.float32)
    block_out = (found.astype(jnp.float32) + mixed_all).astype(jnp.bfloat16)
    return (in_new, out_new, block_out, window_state, state)


def solution(mesh):
    placed = (
        P(("fsdp", "chan"), None, None),
        P(("fsdp", "chan"), None, None),
        P(("fsdp", "chan"), None, None),
        P(("fsdp", "chan"), None, None),
        P(("fsdp", "chan"), None),
        P(("fsdp", "chan"), None),
        P(("fsdp", "chan"), None),
        P(("fsdp", "chan"), None),
        P("fsdp", "chan"),
        P(None, "fsdp"),
        P("fsdp", None, "chan"),
        P("fsdp", None, "chan"),
        P(None, "chan"),
        P("chan"),
        P(None, "chan"),
        P("chan", None),
        P("chan"),
        P(None, "chan"),
        P("chan"),
    )
    return jax.shard_map(
        per_device,
        mesh=mesh,
        in_specs=placed,
        out_specs=(
            P(("fsdp", "chan"), None, None),
            P(("fsdp", "chan"), None),
            P(None, "fsdp", "chan"),
            P("fsdp", None, "chan"),
            P("fsdp", None, "chan"),
        ),
        check_vma=False,
    )
```

profile of v0, /device:TPU:0, one launch (start us, length us, event | category | flops | bytes accessed | tf_op | source)
XLA Modules:
  0.0 634.5 jit_solution(9839498305490577094)
XLA Ops:
  17.2 5.8 fusion.65
  23.1 7.2 %copy.53 = f32[128,2,4096]{0,2,1:T(8,128)} copy(f32[128,2,4096]{2,1,0:T(2,128)} %param.19) | data formatting | bytes 8388608 | tf_op args[0]
  30.3 7.4 %copy.51 = f32[128,2,4096]{0,2,1:T(8,128)} copy(f32[128,2,4096]{2,1,0:T(2,128)} %param.21) | data formatting | bytes 8388608 | tf_op args[2]
  37.7 6.2 copy.50
  43.9 7.3 %copy.49 = f32[128,2,4096]{0,2,1:T(8,128)} copy(f32[128,2,4096]{2,1,0:T(2,128)} %param.20) | data formatting | bytes 8388608 | tf_op args[1]
  51.2 8.4 %fusion.63 = (bf16[128,2,4096]{0,2,1:T(8,128)(2,1)S(1)}, f32[128,2,4096]{0,2,1:T(8,128)}) fusion(f32[128,2,4096]{0,2,1:T(8,128)} %copy.53, f32[128,2,4096]{0,2,1:T(8,128)} %copy.51, bf16[128,2,4096]{0,2,1:T(8,128)(2,1)} %copy.50, f32[128,2,4096]{0,2,1:T(8,128)} %copy.49), kind=kLoop, calls=%fused_computation.141 | loop fusion | flops 17825792 | bytes 20971520 | tf_op jit(solution)/shard_map/convert.5
  61.9 25.0 %all_gather.15 = s32[4,1024]{1,0:T(4,128)S(1)} all-gather(s32[4,128]{1,0:T(4,128)S(1)} %copy-done.24), channel_id=1, replica_groups=mesh['fsdp'=8,'chan'=4] {'fsdp'}, dimensions={1}, use_global_device_ids=true | all-gather | bytes 18432 | tf_op jit(solution)/shard_map/all_gather | solution.py:77
  87.0 28.8 %gather_fusion = bf16[4096,1024]{1,0:T(8,128)(2,1)} fusion(bf16[8192,1024]{1,0:T(8,128)(2,1)} %param.27, s32[4096]{0:T(1024)S(1)} %bitcast_clamp_fusion), kind=kCustom, calls=%fused_computation | custom fusion | bytes 16793600 | tf_op jit(solution)/shard_map/jit(_take)/gather | solution.py:80
  115.8 7.9 %select_select_fusion = bf16[4,1024,1024]{2,1,0:T(8,128)(2,1)} fusion(bf16[4,1024,1024]{2,1,0:T(8,128)(2,1)} %bitcast.69, pred[4,1024]{1,0:T(4,128)(4,1)S(1)} %get-tuple-element.53, pred[4,1024]{1,0:T(4,128)(4,1)S(1)} %get-tuple-element.52), kind=kLoop, calls=%fused_computation.13 | loop fusion | flops 8388608 | bytes 16785408 | tf_op jit(solution)/shard_map/jit(_where)/select_n | solution.py:81
  123.7 5.6 all-to-all-start.2
  129.4 62.1 %all-gather.13.cloned.1.call-done = bf16[1024,1,4096]{0,2,1:T(8,128)(2,1)} async-done(((bf16[128,1,4096]{0,2,1:T(8,128)(2,1)}), bf16[1024,1,4096]{0,2,1:T(8,128)(2,1)}) %all-gather.13.cloned.1.call-update) | async-done | bytes 8388624 | tf_op jit(solution)/shard_map/all_gather | solution.py:65
  191.4 31.0 %all-to-all-done.2 = bf16[1024,4,1024]{0,2,1:T(8,128)(2,1)} async-done(((bf16[1024,4,1024]{0,2,1:T(8,128)(2,1)}), bf16[1024,4,1024]{0,2,1:T(8,128)(2,1)}, u32[]{:S(2)}, u32[]{:S(2)}) %all-to-all-start.2) | async-done | bytes 8388640 | tf_op jit(solution)/shard_map/all_to_all | solution.py:71
  222.5 5.7 all-to-all-start.1
  228.2 46.1 %all-gather.11.cloned.1.call-done = bf16[1024,1,4096]{0,2,1:T(8,128)(2,1)} async-done(((bf16[128,1,4096]{0,2,1:T(8,128)(2,1)}), bf16[1024,1,4096]{0,2,1:T(8,128)(2,1)}) %all-gather.11.cloned.1.call-update) | async-done | bytes 8388624 | tf_op jit(solution)/shard_map/all_gather | solution.py:64
  274.3 46.1 %all-to-all-done.1 = bf16[1024,4,1024]{0,2,1:T(8,128)(2,1)} async-done(((bf16[1024,4,1024]{0,2,1:T(8,128)(2,1)}), bf16[1024,4,1024]{0,2,1:T(8,128)(2,1)}, u32[]{:S(2)}, u32[]{:S(2)}) %all-to-all-start.1) | async-done | bytes 8388640 | tf_op jit(solution)/shard_map/all_to_all | solution.py:70
  320.4 5.8 all-to-all-start
  326.3 38.5 %reduce-scatter.3.cloned.1.call-done = bf16[4,128,1024]{2,1,0:T(8,128)(2,1)} async-done(((bf16[4,1024,1024]{2,1,0:T(8,128)(2,1)}), bf16[4,128,1024]{2,1,0:T(8,128)(2,1)}) %reduce-scatter.3.cloned.1.call-update) | async-done | bytes 1048592 | tf_op jit(solution)/shard_map/reduce_scatter | solution.py:83
  365.3 11.6 %copy.69 = bf16[4,1024,1024]{2,1,0:T(8,128)(2,1)} copy(bf16[4,1024,1024]{1,2,0:T(8,128)(2,1)} %bitcast.19) | data formatting | bytes 16777216 | tf_op jit(solution)/shard_map/all_to_all | solution.py:71
  376.9 8.2 %copy.70 = bf16[8,4,128,1024]{3,2,1,0:T(8,128)(2,1)} copy(bf16[8,4,128,1024]{3,2,0,1:T(8,128)(2,1)} %bitcast.70) | data formatting | bytes 16777216 | tf_op jit(solution)/shard_map/transpose | solution.py:30
  385.1 8.9 %copy.75 = bf16[512,8,8,128]{3,2,1,0:T(8,128)(2,1)} copy(bf16[512,8,8,128]{3,1,2,0:T(8,128)(2,1)} %bitcast.38) | data formatting | bytes 16777216
  394.1 12.2 %copy.62 = bf16[4,8,128,1024]{3,2,0,1:T(8,128)(2,1)} copy(bf16[4,8,128,1024]{2,1,3,0:T(8,128)(2,1)} %bitcast.71) | data formatting | bytes 16777216 | tf_op jit(solution)/shard_map/reshape | solution.py:29
  406.2 23.1 %all-to-all-done = bf16[1024,4,1024]{0,2,1:T(8,128)(2,1)} async-done(((bf16[1024,4,1024]{0,2,1:T(8,128)(2,1)}), bf16[1024,4,1024]{0,2,1:T(8,128)(2,1)}, u32[]{:S(2)}, u32[]{:S(2)}) %all-to-all-start) | async-done | bytes 8388640 | tf_op jit(solution)/shard_map/all_to_all | solution.py:69
  429.3 9.2 %copy.74 = bf16[512,8,8,128]{3,2,1,0:T(8,128)(2,1)} copy(bf16[512,8,8,128]{3,1,2,0:T(8,128)(2,1)} %bitcast.32) | data formatting | bytes 16777216
  438.6 12.3 %copy.59 = bf16[4,8,128,1024]{3,2,0,1:T(8,128)(2,1)} copy(bf16[4,8,128,1024]{2,1,3,0:T(8,128)(2,1)} %bitcast.72) | data formatting | bytes 16777216 | tf_op jit(solution)/shard_map/reshape | solution.py:29
  450.9 6.1 all-gather.7.cloned.1.call-done
  465.3 4.5 convolution_convert_fusion.2
  477.5 10.2 %convolution_convert_fusion.1 = bf16[512,1024]{1,0:T(8,128)(2,1)} fusion(bf16[512,4096]{1,0:T(8,128)(2,1)} %bitcast.82, bf16[4096,1024]{1,0:T(8,128)(2,1)} %bitcast.79), kind=kOutput, calls=%fused_computation.48 | convolution fusion | flops 4295491584 | bytes 13631488 | tf_op jit(solution)/shard_map/dot_general | solution.py:99
  487.7 35.9 %all-reduce.3.cloned.1.call-done = (f32[128,288]{0,1:T(8,128)}, f32[128,288]{0,1:T(8,128)}, f32[128,288]{0,1:T(8,128)}, f32[128,288]{0,1:T(8,128)}) async-done(((f32[128,288]{0,1:T(8,128)}, f32[128,288]{0,1:T(8,128)}, f32[128,288]{0,1:T(8,128)}, f32[128,288]{0,1:T(8,128)}), (f32[128,288]{0,1:T(8,128)}, f32[128,288]{0,1:T(8,128)}, f32[128,288]{0,1:T(8,128)}, ...) | async-done | bytes 589840 | tf_op jit(solution)/shard_map/psum | solution.py:115
  546.1 17.0 %multiply_reduce_fusion.2 = (f32[128,1024]{1,0:T(8,128)S(1)}, f32[128,1024]{1,0:T(8,128)S(1)}, f32[128,1024]{1,0:T(8,128)S(1)}, f32[128,1024]{1,0:T(8,128)S(1)}, f32[128,16,1024]{2,1,0:T(8,128)}) fusion(f32[128,16]{1,0:T(8,128)} %copy.63, f32[128,16]{1,0:T(8,128)} %copy.64, f32[128,1024]{1,0:T(8,128)} %get-tuple-element.58, f32[128,16]{1,0:T(8,128)} %copy.61, ...), kind=kLoop, calls=%fused_computation.9 | loop fusion | flops 49807360 | bytes 23199744 | tf_op jit(solution)/shard_map/reduce_sum | solution.py:128
  564.7 7.1 %convolution_convert_fusion = bf16[4,128,4096]{2,1,0:T(8,128)(2,1)} fusion(bf16[4096,1024,1]{1,0,2:T(8,128)(2,1)S(1)} %bitcast.75, bf16[1,128,1024]{2,1,0:T(8,128)(2,1)S(1)} %get-tuple-element.37, bf16[1,128,1024]{2,1,0:T(8,128)(2,1)S(1)} %get-tuple-element.38, bf16[1,128,1024]{2,1,0:T(8,128)(2,1)} %get-tuple-element.39, ...), kind=kOutput, calls=%fused_computation.15 | convolution fusion | flops 4298637312 | bytes 13631488 | tf_op jit(solution)/shard_map/dot_general | solution.py:133
  571.8 7.2 %copy.71 = f32[128,2,4096]{2,1,0:T(2,128)} copy(f32[128,2,4096]{0,2,1:T(8,128)} %get-tuple-element.29) | data formatting | bytes 8388608
  582.7 41.8 %reduce-scatter.5.cloned.1.call-done = bf16[4,128,1024]{2,1,0:T(8,128)(2,1)} async-done(((bf16[4,128,4096]{2,1,0:T(8,128)(2,1)}), bf16[4,128,1024]{2,1,0:T(8,128)(2,1)}) %reduce-scatter.5.cloned.1.call-update) | async-done | bytes 1048592 | tf_op jit(solution)/shard_map/reduce_scatter | solution.py:136
  (110 shorter events, 59.4 us)
Async XLA Ops:
  7.2 466.1 %copy-start = (bf16[288,1024]{1,0:T(8,128)(2,1)S(1)}, bf16[288,1024]{1,0:T(8,128)(2,1)}, u32[]{:S(2)}) copy-start(bf16[288,1024]{1,0:T(8,128)(2,1)} %param.33) | copy-start | bytes 1769476
  7.2 3.1 copy-start.16
  7.2 116.5 %all-gather.9.cloned.1.call-start = ((), (), s32[]{:S(2)}) async-start(), calls=%async_computation.7 | async-start | bytes 9437184 | tf_op jit(solution)/shard_map/all_gather | solution.py:66
  23.1 168.3 %all-gather.13.cloned.1.call-start = ((), (), s32[]{:S(2)}) async-start(), calls=%async_computation.10 | async-start | bytes 9437184 | tf_op jit(solution)/shard_map/all_gather | solution.py:65
  59.7 2.3 copy-start.24
  61.1 213.2 %all-gather.11.cloned.1.call-start = ((), (), s32[]{:S(2)}) async-start(), calls=%async_computation.9 | async-start | bytes 9437184 | tf_op jit(solution)/shard_map/all_gather | solution.py:64
  61.9 302.9 %reduce-scatter.3.cloned.1.call-start = ((), (), s32[]{:S(2)}) async-start(), calls=%async_computation.5 | async-start | bytes 9437184 | tf_op jit(solution)/shard_map/reduce_scatter | solution.py:83
  123.7 98.7 %all-to-all-start.2 = ((bf16[1024,4,1024]{0,2,1:T(8,128)(2,1)}), bf16[1024,4,1024]{0,2,1:T(8,128)(2,1)}, u32[]{:S(2)}, u32[]{:S(2)}) async-start(bf16[1024,4,1024]{0,2,1:T(8,128)(2,1)} %bitcast.77), calls=%async_computation.3 | async-start | bytes 16777216 | tf_op jit(solution)/shard_map/all_to_all | solution.py:71
  222.5 97.9 %all-to-all-start.1 = ((bf16[1024,4,1024]{0,2,1:T(8,128)(2,1)}), bf16[1024,4,1024]{0,2,1:T(8,128)(2,1)}, u32[]{:S(2)}, u32[]{:S(2)}) async-start(bf16[1024,4,1024]{0,2,1:T(8,128)(2,1)} %bitcast.78), calls=%async_computation.2 | async-start | bytes 16777216 | tf_op jit(solution)/shard_map/all_to_all | solution.py:70
  320.4 44.9 %copy-start.20 = (f32[16,1024]{1,0:T(8,128)S(1)}, f32[16,1024]{1,0:T(8,128)}, u32[]{:S(2)}) copy-start(f32[16,1024]{1,0:T(8,128)} %param.36) | copy-start | bytes 196612
  320.4 108.9 %all-to-all-start = ((bf16[1024,4,1024]{0,2,1:T(8,128)(2,1)}), bf16[1024,4,1024]{0,2,1:T(8,128)(2,1)}, u32[]{:S(2)}, u32[]{:S(2)}) async-start(bf16[1024,4,1024]{0,2,1:T(8,128)(2,1)} %bitcast.76), calls=%async_computation.1 | async-start | bytes 16777216 | tf_op jit(solution)/shard_map/all_to_all | solution.py:69
  326.3 130.7 %all-gather.7.cloned.1.call-start = ((), (), s32[]{:S(2)}) async-start(), calls=%async_computation.6 | async-start | bytes 5242880 | tf_op jit(solution)/shard_map/all_gather | solution.py:87
  364.8 158.8 %all-reduce.3.cloned.1.call-start = ((), (), s32[]{:S(2)}) async-start(), calls=%async_computation.11 | async-start | bytes 1179648 | tf_op jit(solution)/shard_map/psum | solution.py:115
  457.0 3.4 copy-start.1
  460.4 4.9 copy-start.2
  461.9 7.9 %copy-start.6 = (bf16[4,128,4096]{2,1,0:T(8,128)(2,1)}, bf16[4,128,4096]{2,1,0:T(8,128)(2,1)S(1)}, u32[]{:S(2)}) copy-start(bf16[4,128,4096]{2,1,0:T(8,128)(2,1)S(1)} %fusion.1) | copy-start | bytes 12582916
  465.3 4.6 copy-start.14
  470.2 2.4 copy-start.4
  472.6 4.9 copy-start.7
  472.6 4.9 copy-start.9
  477.2 147.3 %reduce-scatter.5.cloned.1.call-start = ((), (), s32[]{:S(2)}) async-start(), calls=%async_computation.8 | async-start | bytes 5242880 | tf_op jit(solution)/shard_map/reduce_scatter | solution.py:136
  477.5 47.5 %copy-start.3 = (bf16[1024,256]{1,0:T(8,128)(2,1)S(1)}, bf16[1024,256]{1,0:T(8,128)(2,1)}, u32[]{:S(2)}) copy-start(bf16[1024,256]{1,0:T(8,128)(2,1)} %param.34) | copy-start | bytes 1572868
  477.5 47.5 %copy-start.19 = (f32[1024]{0:T(1024)S(1)}, f32[1024]{0:T(1024)}, u32[]{:S(2)}) copy-start(f32[1024]{0:T(1024)} %param.35) | copy-start | bytes 12292
  523.6 8.9 %copy-start.18 = (f32[128,288]{0,1:T(8,128)S(1)}, f32[128,288]{0,1:T(8,128)}, u32[]{:S(2)}) copy-start(f32[128,288]{0,1:T(8,128)} %get-tuple-element.22) | copy-start | bytes 442372
  523.6 10.3 %copy-start.12 = (bf16[128,1024]{1,0:T(8,128)(2,1)S(1)}, bf16[128,1024]{1,0:T(8,128)(2,1)}, u32[]{:S(2)}) copy-start(bf16[128,1024]{1,0:T(8,128)(2,1)} %copy-done.11) | copy-start | bytes 786436
  546.1 18.6 %slice-start = ((s8[8388608]{0:T(1024)(128)(4,1)}), s8[4194304]{0:T(1024)(128)(4,1)S(1)}, s32[]{:S(2)}) async-start(s8[8388608]{0:T(1024)(128)(4,1)} %bitcast.73), calls=%async_computation.12 | async-start | bytes 8388608
  546.1 17.0 %copy-start.8 = (bf16[128,1024]{1,0:T(8,128)(2,1)S(1)}, bf16[128,1024]{1,0:T(8,128)(2,1)}, u32[]{:S(2)}) copy-start(bf16[128,1024]{1,0:T(8,128)(2,1)} %copy-done.7) | copy-start | bytes 786436
  546.1 17.0 %copy-start.10 = (bf16[128,1024]{1,0:T(8,128)(2,1)S(1)}, bf16[128,1024]{1,0:T(8,128)(2,1)}, u32[]{:S(2)}) copy-start(bf16[128,1024]{1,0:T(8,128)(2,1)} %copy-done.9) | copy-start | bytes 786436
  546.1 17.1 %copy-start.13 = (bf16[128,1024]{1,0:T(8,128)(2,1)S(1)}, bf16[128,1024]{1,0:T(8,128)(2,1)}, u32[]{:S(2)}) copy-start(bf16[128,1024]{1,0:T(8,128)(2,1)} %copy-done.11) | copy-start | bytes 786436
  546.1 17.1 %copy-start.17 = (bf16[512,1024]{1,0:T(8,128)(2,1)S(1)}, bf16[512,1024]{1,0:T(8,128)(2,1)}, u32[]{:S(2)}) copy-start(bf16[512,1024]{1,0:T(8,128)(2,1)} %convolution_convert_fusion.1) | copy-start | bytes 3145732
  546.1 17.1 %copy-start.23 = (f32[1024]{0:T(1024)S(1)}, f32[1024]{0:T(1024)}, u32[]{:S(2)}) copy-start(f32[1024]{0:T(1024)} %param.37) | copy-start | bytes 12292
  546.1 18.6 %slice-start.1 = ((s8[8388608]{0:T(1024)(128)(4,1)}), s8[4194304]{0:T(1024)(128)(4,1)S(1)}, s32[]{:S(2)}) async-start(s8[8388608]{0:T(1024)(128)(4,1)} %bitcast.73), calls=%async_computation.13 | async-start | bytes 8388608
  (5 other events, 7.1 us)
Sparse Core Ops, SparseCore 0:
  23.2 85.2 all-gather.8
  110.7 80.6 all-gather.12
  193.6 80.6 all-gather.10
  277.0 87.6 reduce-scatter.2
  366.4 90.4 all-gather.6
  477.4 46.2 all-reduce.2
  571.9 52.5 reduce-scatter.4
where the time goes:
time: 645 us; the launch traced here: 635 us
  waiting for transfers between devices  332 us (51%)
  local copies, waits for them, and re-layouts  158 us (24%)
  other arithmetic  52.4 us (8%)
  matrix products  34.7 us (5%)
  blocking collectives  25 us (4%)
  starting transfers between devices  18.1 us (3%)
  between operations  14.8 us (2%)
    unnamed x66, local copies, waits for them, and re-layouts  70 us
    all_gather x1, waiting for transfers between devices, per_device(): lax.all_gather(pieces[1], 'fsdp', axis=0, tiled=True)  62.1 us
    all_gather x1, waiting for transfers between devices, per_device(): lax.all_gather(pieces[0], 'fsdp', axis=0, tiled=True)  46.1 us
    all_to_all x1, waiting for transfers between devices, per_device(): lax.all_to_all(stacked[1], 'chan', split_axis=1, concat_axis=0, tiled=True)  46.1 us
    reduce_scatter x1, waiting for transfers between devices, per_device(): lax.psum_scatter(terms.astype(jnp.bfloat16), 'chan', scatter_dimension=2,...  41.8 us
    reduce_scatter x1, waiting for transfers between devices, per_device(): lax.psum_scatter(picked, 'fsdp', scatter_dimension=1, tiled=True)  38.5 us
    psum x1, waiting for transfers between devices, per_device(): dbc = lax.psum(partial_value, 'chan')  35.9 us
    all_to_all x1, waiting for transfers between devices, per_device(): lax.all_to_all(stacked[2], 'chan', split_axis=1, concat_axis=0, tiled=True)  31 us
  transfers between devices with their start and end apart: 10, of which 9 were waited for; matrix products, arithmetic and copies ran while one was open for 25% of the time, Pallas kernels for 0%

commit v1 on v0

--- a/solution.py
+++ b/solution.py
@@ -14,6 +14,12 @@
 bias_first = 1.0 - math.pow(0.8, 10)
 bias_second = 1.0 - math.pow(0.95, 10)
 norm_eps = 1e-06
+
+
+def stacked_exchange(x, mesh_axis, split, join):
+    pieces = jnp.split(x, lax.axis_size(mesh_axis), axis=split)
+    arrived = lax.all_to_all(jnp.stack(pieces), mesh_axis, 0, 0)
+    return jnp.concatenate(arrived, axis=join)
 
 
 def adam_update(master, moment, velocity, grad):
@@ -68,7 +74,7 @@
     spread = (
         lax.all_to_all(stacked[0], "chan", split_axis=1, concat_axis=0, tiled=True),
         lax.all_to_all(stacked[1], "chan", split_axis=1, concat_axis=0, tiled=True),
-        lax.all_to_all(stacked[2], "chan", split_axis=1, concat_axis=0, tiled=True),
+        stacked_exchange(stacked[2], "chan", 1, 0),
     )
     relay_x = reorder_rows(spread[0], groups, replicas)
     relay_z = reorder_rows(spread[1], groups, replicas)

time: 645 us -> 614 us (0.952); the launches traced: 635 us -> 612 us
  local copies, waits for them, and re-layouts: 158 us -> 127 us
  waiting for transfers between devices: 332 us -> 349 us
  blocking collectives: 25 us -> 16 us
    unnamed x66 -> x41, local copies, waits for them, and re-layouts: 70 us -> 56.4 us
    another operation x0 -> x2, local copies, waits for them, and re-layouts: none -> 13 us  [the longest x1 8.58 us: reorder_rows(): shaped = block.reshape(groups, replicas, -1, width)]
    all_to_all x1 -> x0, local copies, waits for them, and re-layouts: 11.6 us -> none  [per_device(): lax.all_to_all(stacked[2], 'chan', split_axis=1, concat_axis=0, tiled=True)]
    all_to_all x1, waiting for transfers between devices: 23.1 us -> 33 us  [per_device(): lax.all_to_all(stacked[0], 'chan', split_axis=1, concat_axis=0, tiled=True)]
    all_gather x1, blocking collectives: 25 us -> 16 us  [per_device(): every_token = lax.all_gather(tokens, 'fsdp', axis=1, tiled=True)]
    transpose x1 -> x0, local copies, waits for them, and re-layouts: 8.25 us -> none  [reorder_rows(): return jnp.transpose(shaped, (1, 0, 2, 3)).reshape(-1, width)]
where the time goes in v1:
time: 614 us; the launch traced here: 612 us
  waiting for transfers between devices  349 us (57%)
  local copies, waits for them, and re-layouts  127 us (21%)
  other arithmetic  53.9 us (9%)
  matrix products  33.7 us (5%)
  starting transfers between devices  17.8 us (3%)
  blocking collectives  16 us (3%)
  between operations  14.5 us (2%)
    all_gather x1, waiting for transfers between devices, per_device(): lax.all_gather(pieces[1], 'fsdp', axis=0, tiled=True)  64.1 us
    unnamed x41, local copies, waits for them, and re-layouts  56.4 us
    all_gather x1, waiting for transfers between devices, per_device(): lax.all_gather(pieces[0], 'fsdp', axis=0, tiled=True)  48.1 us
    reduce_scatter x1, waiting for transfers between devices, per_device(): lax.psum_scatter(terms.astype(jnp.bfloat16), 'chan', scatter_dimension=2,...  44.5 us
    all_to_all x1, waiting for transfers between devices, per_device(): lax.all_to_all(stacked[1], 'chan', split_axis=1, concat_axis=0, tiled=True)  44.2 us
    reduce_scatter x1, waiting for transfers between devices, per_device(): lax.psum_scatter(picked, 'fsdp', scatter_dimension=1, tiled=True)  39.8 us
    psum x1, waiting for transfers between devices, per_device(): dbc = lax.psum(partial_value, 'chan')  35.9 us
    all_to_all x1, waiting for transfers between devices, per_device(): lax.all_to_all(stacked[0], 'chan', split_axis=1, concat_axis=0, tiled=True)  33 us
  transfers between devices with their start and end apart: 10, of which 9 were waited for; matrix products, arithmetic and copies ran while one was open for 25% of the time, Pallas kernels for 0%

profile of v1, /device:TPU:0, one launch (start us, length us, event | category | flops | bytes accessed | tf_op | source)
XLA Modules:
  0.0 611.9 jit_solution(9844813553168000914)
XLA Ops:
  7.2 6.5 %fusion.65 = (bf16[128,4096]{1,0:T(8,128)(2,1)}, f32[128,4096]{1,0:T(8,128)}) fusion(f32[128,4096]{1,0:T(8,128)} %param.23, f32[128,4096]{1,0:T(8,128)} %param.25, bf16[128,4096]{1,0:T(8,128)(2,1)} %param.26, f32[128,4096]{1,0:T(8,128)} %param.24), kind=kLoop, calls=%fused_computation.147 | loop fusion | flops 8912896 | bytes 10485760 | tf_op jit(solution)/shard_map/convert_element_type | solution.py:65
  13.8 7.2 %copy.37 = f32[128,2,4096]{0,2,1:T(8,128)} copy(f32[128,2,4096]{2,1,0:T(2,128)} %param.19) | data formatting | bytes 8388608 | tf_op args[0]
  21.1 7.4 %copy.35 = f32[128,2,4096]{0,2,1:T(8,128)} copy(f32[128,2,4096]{2,1,0:T(2,128)} %param.21) | data formatting | bytes 8388608 | tf_op args[2]
  28.5 4.9 copy.34
  33.4 7.3 %copy.33 = f32[128,2,4096]{0,2,1:T(8,128)} copy(f32[128,2,4096]{2,1,0:T(2,128)} %param.20) | data formatting | bytes 8388608 | tf_op args[1]
  40.7 7.9 %fusion.63 = (bf16[128,2,4096]{0,2,1:T(8,128)(2,1)S(1)}, f32[128,2,4096]{0,2,1:T(8,128)}) fusion(f32[128,2,4096]{0,2,1:T(8,128)} %copy.37, f32[128,2,4096]{0,2,1:T(8,128)} %copy.35, bf16[128,2,4096]{0,2,1:T(8,128)(2,1)S(1)} %copy.34, f32[128,2,4096]{0,2,1:T(8,128)} %copy.33), kind=kLoop, calls=%fused_computation.146 | loop fusion | flops 17825792 | bytes 20971520 | tf_op jit(solution)/shard_map/convert.5
  50.9 16.0 %all_gather.15 = s32[4,1024]{1,0:T(4,128)S(1)} all-gather(s32[4,128]{1,0:T(4,128)S(1)} %copy-done.14), channel_id=1, replica_groups=mesh['fsdp'=8,'chan'=4] {'fsdp'}, dimensions={1}, use_global_device_ids=true | all-gather | bytes 18432 | tf_op jit(solution)/shard_map/all_gather | solution.py:83
  66.9 28.9 %gather_fusion = bf16[4096,1024]{1,0:T(8,128)(2,1)} fusion(bf16[8192,1024]{1,0:T(8,128)(2,1)} %param.27, s32[4096]{0:T(1024)S(1)} %bitcast_clamp_fusion), kind=kCustom, calls=%fused_computation | custom fusion | bytes 16793600 | tf_op jit(solution)/shard_map/jit(_take)/gather | solution.py:86
  95.8 7.6 %select_select_fusion = bf16[4,1024,1024]{2,1,0:T(8,128)(2,1)} fusion(bf16[4,1024,1024]{2,1,0:T(8,128)(2,1)} %bitcast.75, pred[4,1024]{1,0:T(4,128)(4,1)S(1)} %get-tuple-element.52, pred[4,1024]{1,0:T(4,128)(4,1)S(1)} %get-tuple-element.51), kind=kLoop, calls=%fused_computation.14 | loop fusion | flops 8388608 | bytes 16785408 | tf_op jit(solution)/shard_map/jit(_where)/select_n | solution.py:87
  103.4 4.4 slice_bitcast_fusion.3
  111.7 5.6 all-to-all-start.2
  117.4 64.1 %all-gather.13.cloned.1.call-done = bf16[1024,1,4096]{0,2,1:T(8,128)(2,1)} async-done(((bf16[128,1,4096]{0,2,1:T(8,128)(2,1)}), bf16[1024,1,4096]{0,2,1:T(8,128)(2,1)}) %all-gather.13.cloned.1.call-update) | async-done | bytes 8388624 | tf_op jit(solution)/shard_map/all_gather | solution.py:71
  181.4 29.1 %all-to-all-done.2 = bf16[4,1024,1024]{2,1,0:T(8,128)(2,1)} async-done(((bf16[4,1024,1024]{2,1,0:T(8,128)(2,1)}), bf16[4,1024,1024]{2,1,0:T(8,128)(2,1)}, u32[]{:S(2)}, u32[]{:S(2)}) %all-to-all-start.2) | async-done | bytes 8388640 | tf_op jit(solution)/shard_map/all_to_all | solution.py:21
  210.5 5.7 all-to-all-start.1
  216.2 48.1 %all-gather.11.cloned.1.call-done = bf16[1024,1,4096]{0,2,1:T(8,128)(2,1)} async-done(((bf16[128,1,4096]{0,2,1:T(8,128)(2,1)}), bf16[1024,1,4096]{0,2,1:T(8,128)(2,1)}) %all-gather.11.cloned.1.call-update) | async-done | bytes 8388624 | tf_op jit(solution)/shard_map/all_gather | solution.py:70
  264.3 44.2 %all-to-all-done.1 = bf16[1024,4,1024]{0,2,1:T(8,128)(2,1)} async-done(((bf16[1024,4,1024]{0,2,1:T(8,128)(2,1)}), bf16[1024,4,1024]{0,2,1:T(8,128)(2,1)}, u32[]{:S(2)}, u32[]{:S(2)}) %all-to-all-start.1) | async-done | bytes 8388640 | tf_op jit(solution)/shard_map/all_to_all | solution.py:76
  308.5 5.8 all-to-all-start
  314.4 39.8 %reduce-scatter.3.cloned.1.call-done = bf16[4,128,1024]{2,1,0:T(8,128)(2,1)} async-done(((bf16[4,1024,1024]{2,1,0:T(8,128)(2,1)}), bf16[4,128,1024]{2,1,0:T(8,128)(2,1)}) %reduce-scatter.3.cloned.1.call-update) | async-done | bytes 1048592 | tf_op jit(solution)/shard_map/reduce_scatter | solution.py:89
  354.5 8.6 %copy.48 = bf16[4,8,128,1024]{3,2,0,1:T(8,128)(2,1)} copy(bf16[4,8,128,1024]{3,2,1,0:T(8,128)(2,1)} %bitcast.22) | data formatting | bytes 16777216 | tf_op jit(solution)/shard_map/reshape;reshape | solution.py:35
  363.1 9.2 %copy.52 = bf16[512,8,8,128]{3,2,1,0:T(8,128)(2,1)} copy(bf16[512,8,8,128]{3,1,2,0:T(8,128)(2,1)} %bitcast.40) | data formatting | bytes 16777216
  372.2 12.3 %copy.41 = bf16[4,8,128,1024]{3,2,0,1:T(8,128)(2,1)} copy(bf16[4,8,128,1024]{2,1,3,0:T(8,128)(2,1)} %bitcast.76) | data formatting | bytes 16777216 | tf_op jit(solution)/shard_map/reshape | solution.py:35
  384.5 33.0 %all-to-all-done = bf16[1024,4,1024]{0,2,1:T(8,128)(2,1)} async-done(((bf16[1024,4,1024]{0,2,1:T(8,128)(2,1)}), bf16[1024,4,1024]{0,2,1:T(8,128)(2,1)}, u32[]{:S(2)}, u32[]{:S(2)}) %all-to-all-start) | async-done | bytes 8388640 | tf_op jit(solution)/shard_map/all_to_all | solution.py:75
  417.5 9.0 %copy.51 = bf16[512,8,8,128]{3,2,1,0:T(8,128)(2,1)} copy(bf16[512,8,8,128]{3,1,2,0:T(8,128)(2,1)} %bitcast.34) | data formatting | bytes 16777216
  426.5 12.2 %copy.38 = bf16[4,8,128,1024]{3,2,0,1:T(8,128)(2,1)} copy(bf16[4,8,128,1024]{2,1,3,0:T(8,128)(2,1)} %bitcast.77) | data formatting | bytes 16777216 | tf_op jit(solution)/shard_map/reshape | solution.py:35
  438.7 10.0 %all-gather.7.cloned.1.call-done = bf16[4,128,4096]{2,1,0:T(8,128)(2,1)} async-done(((bf16[4,128,1024]{2,1,0:T(8,128)(2,1)}), bf16[4,128,4096]{2,1,0:T(8,128)(2,1)}) %all-gather.7.cloned.1.call-update) | async-done | bytes 4194320 | tf_op jit(solution)/shard_map/all_gather | solution.py:93
  457.1 4.5 convolution_convert_fusion.2
  468.5 10.2 %convolution_convert_fusion.1 = bf16[512,1024]{1,0:T(8,128)(2,1)} fusion(bf16[512,4096]{1,0:T(8,128)(2,1)} %bitcast.86, bf16[4096,1024]{1,0:T(8,128)(2,1)} %bitcast.83), kind=kOutput, calls=%fused_computation.53 | convolution fusion | flops 4295491584 | bytes 13631488 | tf_op jit(solution)/shard_map/dot_general | solution.py:105
  478.7 35.9 %all-reduce.3.cloned.1.call-done = (f32[128,288]{0,1:T(8,128)}, f32[128,288]{0,1:T(8,128)}, f32[128,288]{0,1:T(8,128)}, f32[128,288]{0,1:T(8,128)}) async-done(((f32[128,288]{0,1:T(8,128)}, f32[128,288]{0,1:T(8,128)}, f32[128,288]{0,1:T(8,128)}, f32[128,288]{0,1:T(8,128)}), (f32[128,288]{0,1:T(8,128)}, f32[128,288]{0,1:T(8,128)}, f32[128,288]{0,1:T(8,128)}, ...) | async-done | bytes 589840 | tf_op jit(solution)/shard_map/psum | solution.py:121
  525.8 16.7 %multiply_reduce_fusion.2 = (f32[128,1024]{1,0:T(8,128)S(1)}, f32[128,1024]{1,0:T(8,128)S(1)}, f32[128,1024]{1,0:T(8,128)S(1)}, f32[128,1024]{1,0:T(8,128)S(1)}, f32[128,16,1024]{2,1,0:T(8,128)}) fusion(f32[128,16]{1,0:T(8,128)S(1)} %copy.42, f32[128,16]{1,0:T(8,128)S(1)} %copy.43, f32[128,1024]{1,0:T(8,128)} %get-tuple-element.57, f32[128,16]{1,0:T(8,128)S(1)} %copy.40, ...), kind=kLoop, calls=%fused_computation.10 | loop fusion | flops 49807360 | bytes 23199744 | tf_op jit(solution)/shard_map/reduce_sum | solution.py:134
  543.4 6.2 %convolution_convert_fusion = bf16[4,128,4096]{2,1,0:T(8,128)(2,1)} fusion(bf16[4096,1024,1]{1,0,2:T(8,128)(2,1)S(1)} %bitcast.80, bf16[1,128,1024]{2,1,0:T(8,128)(2,1)S(1)} %get-tuple-element.36, bf16[1,128,1024]{2,1,0:T(8,128)(2,1)S(1)} %get-tuple-element.37, bf16[1,128,1024]{2,1,0:T(8,128)(2,1)S(1)} %get-tuple-element.38, ...), kind=kOutput, calls=%fused_computation.16 | convolution fusion | flops 4298637312 | bytes 13631488 | tf_op jit(solution)/shard_map/dot_general | solution.py:139
  549.7 7.3 %copy.49 = f32[128,2,4096]{2,1,0:T(2,128)} copy(f32[128,2,4096]{0,2,1:T(8,128)} %get-tuple-element.24) | data formatting | bytes 8388608
  558.0 44.5 %reduce-scatter.5.cloned.1.call-done = bf16[4,128,1024]{2,1,0:T(8,128)(2,1)} async-done(((bf16[4,128,4096]{2,1,0:T(8,128)(2,1)}), bf16[4,128,1024]{2,1,0:T(8,128)(2,1)}) %reduce-scatter.5.cloned.1.call-update) | async-done | bytes 1048592 | tf_op jit(solution)/shard_map/reduce_scatter | solution.py:142
  (86 shorter events, 37.3 us)
Async XLA Ops:
  7.2 457.1 %copy-start = (bf16[288,1024]{1,0:T(8,128)(2,1)S(1)}, bf16[288,1024]{1,0:T(8,128)(2,1)}, u32[]{:S(2)}) copy-start(bf16[288,1024]{1,0:T(8,128)(2,1)} %param.33) | copy-start | bytes 1769476
  7.2 96.2 %all-gather.9.cloned.1.call-start = ((), (), s32[]{:S(2)}) async-start(), calls=%async_computation.7 | async-start | bytes 9437184 | tf_op jit(solution)/shard_map/all_gather | solution.py:72
  13.8 167.6 %all-gather.13.cloned.1.call-start = ((), (), s32[]{:S(2)}) async-start(), calls=%async_computation.10 | async-start | bytes 9437184 | tf_op jit(solution)/shard_map/all_gather | solution.py:71
  48.6 2.3 copy-start.14
  50.1 214.2 %all-gather.11.cloned.1.call-start = ((), (), s32[]{:S(2)}) async-start(), calls=%async_computation.9 | async-start | bytes 9437184 | tf_op jit(solution)/shard_map/all_gather | solution.py:70
  50.8 303.4 %reduce-scatter.3.cloned.1.call-start = ((), (), s32[]{:S(2)}) async-start(), calls=%async_computation.5 | async-start | bytes 9437184 | tf_op jit(solution)/shard_map/reduce_scatter | solution.py:89
  111.7 98.8 %all-to-all-start.2 = ((bf16[4,1024,1024]{2,1,0:T(8,128)(2,1)}), bf16[4,1024,1024]{2,1,0:T(8,128)(2,1)}, u32[]{:S(2)}, u32[]{:S(2)}) async-start(bf16[4,1024,1024]{2,1,0:T(8,128)(2,1)} %pad_maximum_fusion), calls=%async_computation.3 | async-start | bytes 16777216 | tf_op jit(solution)/shard_map/all_to_all | solution.py:21
  210.5 98.0 %all-to-all-start.1 = ((bf16[1024,4,1024]{0,2,1:T(8,128)(2,1)}), bf16[1024,4,1024]{0,2,1:T(8,128)(2,1)}, u32[]{:S(2)}, u32[]{:S(2)}) async-start(bf16[1024,4,1024]{0,2,1:T(8,128)(2,1)} %bitcast.82), calls=%async_computation.2 | async-start | bytes 16777216 | tf_op jit(solution)/shard_map/all_to_all | solution.py:76
  308.5 45.9 %copy-start.10 = (f32[16,1024]{1,0:T(8,128)S(1)}, f32[16,1024]{1,0:T(8,128)}, u32[]{:S(2)}) copy-start(f32[16,1024]{1,0:T(8,128)} %param.36) | copy-start | bytes 196612
  308.5 109.0 %all-to-all-start = ((bf16[1024,4,1024]{0,2,1:T(8,128)(2,1)}), bf16[1024,4,1024]{0,2,1:T(8,128)(2,1)}, u32[]{:S(2)}, u32[]{:S(2)}) async-start(bf16[1024,4,1024]{0,2,1:T(8,128)(2,1)} %bitcast.81), calls=%async_computation.1 | async-start | bytes 16777216 | tf_op jit(solution)/shard_map/all_to_all | solution.py:75
  314.4 134.3 %all-gather.7.cloned.1.call-start = ((), (), s32[]{:S(2)}) async-start(), calls=%async_computation.6 | async-start | bytes 5242880 | tf_op jit(solution)/shard_map/all_gather | solution.py:93
  354.2 160.4 %all-reduce.3.cloned.1.call-start = ((), (), s32[]{:S(2)}) async-start(), calls=%async_computation.11 | async-start | bytes 1179648 | tf_op jit(solution)/shard_map/psum | solution.py:121
  448.7 3.4 copy-start.1
  452.2 4.9 copy-start.2
  453.6 7.9 %copy-start.4 = (bf16[4,128,4096]{2,1,0:T(8,128)(2,1)}, bf16[4,128,4096]{2,1,0:T(8,128)(2,1)S(1)}, u32[]{:S(2)}) copy-start(bf16[4,128,4096]{2,1,0:T(8,128)(2,1)S(1)} %fusion.1) | copy-start | bytes 12582916
  457.0 4.6 copy-start.6
  461.6 0.7 copy-start.11
  461.9 1.8 copy-start.12
  468.2 134.2 %reduce-scatter.5.cloned.1.call-start = ((), (), s32[]{:S(2)}) async-start(), calls=%async_computation.8 | async-start | bytes 5242880 | tf_op jit(solution)/shard_map/reduce_scatter | solution.py:142
  468.5 46.9 %copy-start.3 = (bf16[1024,256]{1,0:T(8,128)(2,1)S(1)}, bf16[1024,256]{1,0:T(8,128)(2,1)}, u32[]{:S(2)}) copy-start(bf16[1024,256]{1,0:T(8,128)(2,1)} %param.34) | copy-start | bytes 1572868
  468.5 46.9 %copy-start.9 = (f32[1024]{0:T(1024)S(1)}, f32[1024]{0:T(1024)}, u32[]{:S(2)}) copy-start(f32[1024]{0:T(1024)} %param.35) | copy-start | bytes 12292
  514.6 8.1 %copy-start.8 = (f32[128,288]{0,1:T(8,128)S(1)}, f32[128,288]{0,1:T(8,128)}, u32[]{:S(2)}) copy-start(f32[128,288]{0,1:T(8,128)} %get-tuple-element.17) | copy-start | bytes 442372
  525.8 17.6 %slice-start = ((s8[8388608]{0:T(1024)(128)(4,1)}), s8[4194304]{0:T(1024)(128)(4,1)S(1)}, s32[]{:S(2)}) async-start(s8[8388608]{0:T(1024)(128)(4,1)} %bitcast.78), calls=%async_computation.12 | async-start | bytes 8388608
  525.8 16.8 %copy-start.7 = (bf16[512,1024]{1,0:T(8,128)(2,1)S(1)}, bf16[512,1024]{1,0:T(8,128)(2,1)}, u32[]{:S(2)}) copy-start(bf16[512,1024]{1,0:T(8,128)(2,1)} %convolution_convert_fusion.1) | copy-start | bytes 3145732
  525.8 16.8 %copy-start.13 = (f32[1024]{0:T(1024)S(1)}, f32[1024]{0:T(1024)}, u32[]{:S(2)}) copy-start(f32[1024]{0:T(1024)} %param.37) | copy-start | bytes 12292
  525.8 17.6 %slice-start.1 = ((s8[8388608]{0:T(1024)(128)(4,1)}), s8[4194304]{0:T(1024)(128)(4,1)S(1)}, s32[]{:S(2)}) async-start(s8[8388608]{0:T(1024)(128)(4,1)} %bitcast.78), calls=%async_computation.13 | async-start | bytes 8388608
  549.7 52.7 %copy-start.5 = (bf16[4,128,1024]{2,1,0:T(8,128)(2,1)S(1)}, bf16[4,128,1024]{2,1,0:T(8,128)(2,1)}, u32[]{:S(2)}) copy-start(bf16[4,128,1024]{2,1,0:T(8,128)(2,1)} %reduce-scatter.3.cloned.1.call-done) | copy-start | bytes 3145732
Sparse Core Ops, SparseCore 0:
  13.9 84.8 all-gather.8
  100.4 80.9 all-gather.12
  183.6 80.6 all-gather.10
  266.4 87.6 reduce-scatter.2
  355.9 92.7 all-gather.6
  468.3 46.2 all-reduce.2
  549.8 52.5 reduce-scatter.4
